TPU v7x, 32 devices: a whole 2x2x4 slice. The times are simulated.
32 devices in a mesh: band: 16 (over z, x, core), ga: 2 (over y).
Axes of the slice: x: 2, y: 2, z: 4, core: 2. Of those that a mesh axis runs over, the one named last changes fastest.
Arguments:
- psi: float32 [2, 4096, 65536], P(None, 'band', 'ga'), may hold values from -0.0234375 to 0.0234375
- hx: float32 [2, 256, 65536], P(None, 'band', 'ga'), may hold values from -6 to 6
Outputs:
- h_sub: float32 [2, 4096, 256], P(None, ('band', 'ga'))
All inputs are finite; a program needn't handle non-finite values.
Results may differ from a plain program's by a relative error of at most 0.00007.
Values sent between devices are 32-bit elements; how exact they have to be, the bound alone decides.
A program may use at most 192 MiB of HBM per device.

v0:
```python
import jax
import jax.numpy as jnp
from jax import lax
from jax.sharding import PartitionSpec as P

SHARES = (22, 10)


def contract(left, right):
    return lax.dot_general(
        left,
        right,
        (((1,), (1,)), ((), ())),
        precision=lax.Precision.HIGH,
        preferred_element_type=jnp.float32,
    )


def per_device(psi, hx):
    parts, rows, depth = psi.shape
    unit = depth // sum(SHARES)
    bands = psi.reshape(parts * rows, depth)
    total = None
    first = 0
    pieces = []
    for share in SHARES:
        last = first + share * unit
        piece = lax.all_gather(hx[:, :, first:last], "band", axis=1, tiled=True)
        pieces.append((first, last, piece))
        first = last
    for first, last, piece in pieces:
        product = contract(bands[:, first:last], piece.reshape(-1, last - first))
        total = product if total is None else total + product
    vectors = total.shape[1] // parts
    real_left, imag_left = total[:rows], total[rows:]
    real_tile = real_left[:, :vectors] + imag_left[:, vectors:]
    imag_tile = real_left[:, vectors:] - imag_left[:, :vectors]
    partial_value = jnp.stack([real_tile, imag_tile], axis=0)
    n = lax.axis_size("ga")
    me = lax.axis_index("ga")
    height = rows // n

    def block(owner):
        return lax.dynamic_slice_in_dim(partial_value, owner * height, height, axis=1)

    result = block(me)
    for step in range(1, n):
        ring = [(i, (i + step) % n) for i in range(n)]
        result = result + lax.ppermute(block(lax.rem(me + step, n)), "ga", ring)
    return result


def solution(mesh):
    in_specs = (P(None, "band", "ga"), P(None, "band", "ga"))
    out_specs = P(None, ("band", "ga"), None)
    return jax.shard_map(
        per_device, mesh=mesh, in_specs=in_specs, out_specs=out_specs, check_vma=False
    )
```

profile of v0, /device:TPU:0, one launch (start us, length us, event | category | flops | bytes accessed | tf_op | source)
XLA Modules:
  0.0 389.9 jit_solution(5589482113664164910)
XLA Ops:
  6.5 0.0 all-gather.3.cloned.1.call-start
  6.5 3.6 slice.31
  10.1 0.0 all-gather.3.cloned.1.call-update
  10.2 0.0 all-gather.5.cloned.1.call-start
  10.2 2.5 slice.33
  12.7 0.0 all-gather.5.cloned.1.call-update
  12.7 227.6 %all-gather.3.cloned.1.call-done = f32[2,256,22528]{2,1,0:T(8,128)} async-done(((f32[2,16,22528]{2,1,0:T(8,128)}), f32[2,256,22528]{2,1,0:T(8,128)}) %all-gather.3.cloned.1.call-update) | async-done | bytes 46137360 | tf_op jit(solution)/shard_map/all_gather | solution.py:28
  240.3 43.3 %fusion = f32[512,512]{1,0:T(8,128)S(1)} fusion(f32[512,22528]{1,0:T(8,128)} %bitcast.9, f32[512,32768]{1,0:T(8,128)} %bitcast), kind=kOutput, calls=%fused_computation | convolution fusion | flops 35433480192 | bytes 93323264 | tf_op jit(solution)/shard_map/dot_general | solution.py:10
  283.6 67.1 %all-gather.5.cloned.1.call-done = f32[2,256,10240]{2,1,0:T(8,128)} async-done(((f32[2,16,10240]{2,1,0:T(8,128)}), f32[2,256,10240]{2,1,0:T(8,128)}) %all-gather.5.cloned.1.call-update) | async-done | bytes 20971536 | tf_op jit(solution)/shard_map/all_gather | solution.py:28
  350.7 22.9 %fusion.4 = f32[512,512]{1,0:T(8,128)S(1)} fusion(f32[512,512]{1,0:T(8,128)S(1)} %fusion, f32[512,10240]{1,0:T(8,128)} %bitcast.10, f32[512,32768]{1,0:T(8,128)} %bitcast), kind=kOutput, calls=%fused_computation.4 | convolution fusion | flops 16106389504 | bytes 44040192 | tf_op jit(solution)/shard_map/dot_general | solution.py:10
  373.6 0.1 fusion.10
  373.8 1.5 collective-permute-start
  375.3 7.0 %collective-permute-done = f32[2,128,256]{2,1,0:T(8,128)S(1)} collective-permute-done((f32[2,128,256]{2,1,0:T(8,128)S(1)}, f32[2,128,256]{2,1,0:T(8,128)S(1)}, u32[]{:S(2)}, u32[]{:S(2)}) %collective-permute-start) | collective-permute-done | bytes 262176 | tf_op jit(solution)/shard_map/ppermute | solution.py:49
  382.3 0.7 fusion.9
  (1 shorter events, 0.0 us)
Async XLA Ops:
  6.5 233.8 %all-gather.3.cloned.1.call-start = ((), (), s32[]{:S(2)}) async-start(), calls=%async_computation | async-start | bytes 49020928 | tf_op jit(solution)/shard_map/all_gather | solution.py:28
  10.2 340.5 %all-gather.5.cloned.1.call-start = ((), (), s32[]{:S(2)}) async-start(), calls=%async_computation.1 | async-start | bytes 22282240 | tf_op jit(solution)/shard_map/all_gather | solution.py:28
  373.8 8.5 %collective-permute-start = (f32[2,128,256]{2,1,0:T(8,128)S(1)}, f32[2,128,256]{2,1,0:T(8,128)S(1)}, u32[]{:S(2)}, u32[]{:S(2)}) collective-permute-start(f32[2,128,256]{2,1,0:T(8,128)S(1)} %fusion.7), channel_id=1, source_target_pairs={{0,1},{1,0},{2,3},{3,2},{4,5},{5,4},{6,7},{7,6},{8,9},{9,8},{10,11... | collective-permute-start | bytes 786440 | tf_op jit(solution)/shard_map/ppermute | solution.py:49
Sparse Core Ops, SparseCore 0:
  10.3 230.0 all-gather.2
  241.9 108.7 all-gather.4
where the time goes:
time: 390 us
  waiting for transfers between devices  302 us (77%)
  matrix products  66.2 us (17%)
  between operations  13.4 us (3%)
  local copies, waits for them, and re-layouts  6.08 us (2%)
    all_gather x2, waiting for transfers between devices, per_device(): piece = lax.all_gather(hx[:, :, first:last], 'band', axis=1, tiled=True)  295 us
    dot_general x2, matrix products, contract(): lax.dot_general(left, right, (((1,), (1,)), ((), ())), precision=lax.Prec...  66.2 us
  transfers between devices with their start and end apart: 3, of which 3 were waited for; matrix products, arithmetic and copies ran while one was open for 12% of the time, Pallas kernels for 0%

commit v1 on v0

v1 whole, which is shorter than its diff:
```python
import functools

import jax
import jax.numpy as jnp
from jax import lax
from jax.experimental import pallas as pl
from jax.experimental.pallas import tpu as pltpu
from jax.sharding import PartitionSpec as P

CHUNKS = 8
TILE = 512
SLOTS = 3
MESH = pl.DeviceIdType.MESH


def ladder(mesh):
    chips = mesh.shape["band"] // 2
    try:
        coords = [tuple(mesh.devices[2 * j, 0].coords) for j in range(chips)]
    except AttributeError:
        return 1, 2
    axis = [a != b for a, b in zip(coords[0], coords[1])].index(True)
    if len({c[axis] for c in coords}) == 2:
        return 1, 2
    return chips // 2, 1


def split(x):
    high = x.astype(jnp.bfloat16)
    low = (x - high.astype(jnp.float32)).astype(jnp.bfloat16)
    return high, low


def kernel(
    chips,
    owners,
    strides,
    psi,
    hx,
    out,
    ring,
    twin,
    psi_v,
    hx_v,
    acc,
    final,
    others,
    ring_send,
    ring_recv,
    twin_send,
    twin_recv,
    psi_sem,
    own_sem,
    twin_sem,
    y_send,
    y_recv,
):
    depth = hx.shape[-1]
    half = depth // 2
    width = half // CHUNKS
    rows = psi.shape[1]
    height = rows // owners
    mid = chips // 2
    ticks = chips * CHUNKS
    vectors = hx.shape[1]
    x_stride, z_stride = strides
    long = mid

    me = lax.axis_index("band")
    y = lax.axis_index("ga")
    core = lax.rem(me, 2)
    chip = me // 2
    x = lax.rem(chip // x_stride, 2)
    z = lax.rem(chip // z_stride, long)
    place = z + x * (2 * long - 1 - 2 * z)

    def device_at(position):
        at_x = position // long
        at_z = position + at_x * (2 * long - 1 - 2 * position)
        return 2 * (at_x * x_stride + at_z * z_stride) + core

    after = device_at(lax.rem(place + 1, chips))
    before = device_at(lax.rem(place + chips - 1, chips))
    partner = me + 1 - 2 * core
    target = (after, before)

    def columns(way, c):
        return pl.ds(pl.multiple_of(way * half + c * width, 128), width)

    def with_held(step, way, c, act):
        cols = columns(way, c)
        if isinstance(step, int):
            act(hx.at[:, :, cols] if step == 0 else ring.at[step - 1, :, :, cols])
            return
        pl.when(step == 0)(lambda: act(hx.at[:, :, cols]))
        pl.when(step > 0)(lambda: act(ring.at[step - 1, :, :, cols]))

    def ring_copy(step, way, c, source):
        return pltpu.make_async_remote_copy(
            src_ref=source,
            dst_ref=ring.at[step, :, :, columns(way, c)],
            send_sem=ring_send.at[way, step, c],
            recv_sem=ring_recv.at[way, step, c],
            device_id={"band": target[way]},
            device_id_type=MESH,
        )

    def twin_copy(step, way, c, source):
        return pltpu.make_async_remote_copy(
            src_ref=source,
            dst_ref=twin.at[step, :, :, columns(way, c)],
            send_sem=twin_send.at[way, step, c],
            recv_sem=twin_recv.at[way, step, c],
            device_id={"band": partner},
            device_id_type=MESH,
        )

    def psi_load(t, way):
        c = lax.rem(t, CHUNKS)
        slot = lax.rem(t, SLOTS)
        return pltpu.make_async_copy(
            psi.at[:, :, columns(way, c)], psi_v.at[slot, way], psi_sem.at[slot, way]
        )

    def own_load(t, way, source):
        slot = lax.rem(t, SLOTS)
        return pltpu.make_async_copy(
            source, hx_v.at[slot, way, :, core], own_sem.at[slot, way]
        )

    def twin_load(t, way):
        step, c = t // CHUNKS, lax.rem(t, CHUNKS)
        slot = lax.rem(t, SLOTS)
        return pltpu.make_async_copy(
            twin.at[step, :, :, columns(way, c)],
            hx_v.at[slot, way, :, 1 - core],
            twin_sem.at[slot, way],
        )

    def place_of(step, way):
        late = step // mid
        pair = (1 - late) * step + late * lax.rem(chips - step, mid)
        side = late if way == 0 else lax.rem((step + mid - 1) // mid, 2)
        return 2 * pair + side

    def compute(t, way):
        step, c = t // CHUNKS, lax.rem(t, CHUNKS)
        slot = lax.rem(t, SLOTS)
        own_load(t, way, hx.at[:, :, columns(way, c)]).wait()
        twin_load(t, way).wait()
        psi_load(t, way).wait()
        where = place_of(step, way)
        tile = min(TILE, width)

        def body(k, carry):
            cols = pl.ds(pl.multiple_of(k * tile, 128), tile)
            real = hx_v[slot, way, 0, :, :, cols].reshape(2 * vectors, tile)
            imag = hx_v[slot, way, 1, :, :, cols].reshape(2 * vectors, tile)
            real_high, real_low = split(real)
            imag_high, imag_low = split(imag)
            first = jnp.concatenate([real_high, imag_high, real_low, imag_low], axis=0)
            second = jnp.concatenate(
                [imag_high, -real_high, imag_low, -real_low], axis=0
            )
            total = acc[where]
            for part, right in ((0, first), (1, second)):
                for left in split(psi_v[slot, way, part, :, cols]):
                    total += lax.dot_general(
                        left,
                        right,
                        (((1,), (1,)), ((), ())),
                        preferred_element_type=jnp.float32,
                    )
            acc[where] = total
            return carry

        lax.fori_loop(0, width // tile, body, 0)

    def y_copy(pair, step):
        to = lax.rem(y + step, owners)
        start = pl.multiple_of(to * height, 8)
        return pltpu.make_async_remote_copy(
            src_ref=final.at[pair, pl.ds(start, height)],
            dst_ref=others.at[pair, step - 1],
            send_sem=y_send.at[pair, step - 1],
            recv_sem=y_recv.at[pair, step - 1],
            device_id={"ga": to},
            device_id_type=MESH,
        )

    def finish(step):
        pair = lax.rem(chips - step, mid)
        sides = []
        for side in range(2):
            value = acc[2 * pair + side]
            sides.append(value[:, : 4 * vectors] + value[:, 4 * vectors :])
        final[pair] = jnp.concatenate(sides, axis=1)
        for step_y in range(1, owners):
            y_copy(pair, step_y).start()

    barrier = pltpu.get_barrier_semaphore()
    for neighbour in (after, before, partner):
        pl.semaphore_signal(
            barrier, inc=1, device_id={"band": neighbour}, device_id_type=MESH
        )
    for step_y in range(1, owners):
        pl.semaphore_signal(
            barrier,
            inc=1,
            device_id={"ga": lax.rem(y + step_y, owners)},
            device_id_type=MESH,
        )
    pl.semaphore_wait(barrier, 2 + owners)

    def first_sends(c, carry):
        for way in range(2):
            ring_copy(0, way, c, hx.at[:, :, columns(way, c)]).start()
        return carry

    lax.fori_loop(0, CHUNKS, first_sends, 0)
    acc[...] = jnp.zeros_like(acc)

    def tick(t, carry):
        step, c = t // CHUNKS, lax.rem(t, CHUNKS)

        @pl.when(t < ticks)
        def _():
            for way in range(2):
                psi_load(t, way).start()

        @pl.when(t >= 2)
        def _():
            compute(t - 2, 0)

        @pl.when((t >= 1) & (t <= ticks))
        def _():
            held = t - 1
            held_step, held_c = held // CHUNKS, lax.rem(held, CHUNKS)
            for way in range(2):
                source = hx.at[:, :, columns(way, held_c)]
                twin_copy(held_step, way, held_c, source).wait_recv()
                twin_load(held, way).start()

        @pl.when(t >= 2)
        def _():
            compute(t - 2, 1)
            done = t - 2
            done_step = done // CHUNKS
            pl.when((lax.rem(done, CHUNKS) == CHUNKS - 1) & (done_step >= mid))(
                lambda: finish(done_step)
            )

        @pl.when(t < ticks)
        def _():
            for way in range(2):

                @pl.when(step >= 1)
                def _():
                    source = hx.at[:, :, columns(way, c)]
                    ring_copy(step - 1, way, c, source).wait_recv()

                    @pl.when(step < chips - 1)
                    def _():
                        held = ring.at[step - 1, :, :, columns(way, c)]
                        ring_copy(step, way, c, held).start()

                with_held(
                    step, way, c, lambda ref: twin_copy(step, way, c, ref).start()
                )
                with_held(step, way, c, lambda ref: own_load(t, way, ref).start())

        return carry

    lax.fori_loop(0, ticks + 2, tick, 0)

    def last_waits(t, carry):
        step, c = t // CHUNKS, lax.rem(t, CHUNKS)
        for way in range(2):
            source = hx.at[:, :, columns(way, c)]
            twin_copy(step, way, c, source).wait_send()

            @pl.when(step < chips - 1)
            def _():
                ring_copy(step, way, c, source).wait_send()

        return carry

    lax.fori_loop(0, ticks, last_waits, 0)

    mine = pl.ds(pl.multiple_of(y * height, 8), height)
    for pair in range(mid):
        for step_y in range(1, owners):
            y_copy(pair, step_y).wait_recv()
            final[pair, mine] += others[pair, step_y - 1]
        for step_y in range(1, owners):
            y_copy(pair, step_y).wait_send()

    wide = 2 * vectors
    pieces = [[], []]
    for j in range(chips):
        at_x, at_z = (j // x_stride) % 2, (j // z_stride) % long
        position = at_z + at_x * (2 * long - 1 - 2 * at_z)
        away = lax.rem(place + chips - position, chips)
        late = away // mid
        pair = (1 - late) * away + late * lax.rem(chips - away, mid)
        both = final[pair, mine]
        block = jnp.where(late == 1, both[:, 2 * wide :], both[:, : 2 * wide])
        pieces[0].append(block[:, :wide])
        pieces[1].append(block[:, wide:])
    for part in range(2):
        out[part] = jnp.concatenate(pieces[part], axis=1)


def solution(mesh):
    chips = mesh.shape["band"] // 2
    owners = mesh.shape["ga"]
    strides = ladder(mesh)

    def per_device(psi, hx):
        parts, rows, depth = psi.shape
        vectors = hx.shape[1]
        height = rows // owners
        width = depth // 2 // CHUNKS
        mid = chips // 2
        lanes = 8 * vectors
        dma = pltpu.SemaphoreType.DMA
        result, _, _ = pl.pallas_call(
            functools.partial(kernel, chips, owners, strides),
            out_shape=(
                jax.ShapeDtypeStruct((parts, height, 2 * vectors * chips), jnp.float32),
                jax.ShapeDtypeStruct((chips - 1, *hx.shape), jnp.float32),
                jax.ShapeDtypeStruct((chips, *hx.shape), jnp.float32),
            ),
            in_specs=[pl.BlockSpec(memory_space=pl.ANY)] * 2,
            out_specs=(
                pl.BlockSpec(memory_space=pltpu.VMEM),
                pl.BlockSpec(memory_space=pl.ANY),
                pl.BlockSpec(memory_space=pl.ANY),
            ),
            scratch_shapes=[
                pltpu.VMEM((SLOTS, 2, parts, rows, width), jnp.float32),
                pltpu.VMEM((SLOTS, 2, parts, 2, vectors, width), jnp.float32),
                pltpu.VMEM((chips, rows, lanes), jnp.float32),
                pltpu.VMEM((mid, rows, lanes), jnp.float32),
                pltpu.VMEM((mid, owners - 1, height, lanes), jnp.float32),
                dma((2, chips - 1, CHUNKS)),
                dma((2, chips - 1, CHUNKS)),
                dma((2, chips, CHUNKS)),
                dma((2, chips, CHUNKS)),
                dma((SLOTS, 2)),
                dma((SLOTS, 2)),
                dma((SLOTS, 2)),
                dma((mid, owners - 1)),
                dma((mid, owners - 1)),
            ],
            compiler_params=pltpu.CompilerParams(
                collective_id=0, has_side_effects=True, vmem_limit_bytes=60 * 2**20
            ),
        )(psi, hx)
        return result

    return jax.shard_map(
        per_device,
        mesh=mesh,
        in_specs=(P(None, "band", "ga"), P(None, "band", "ga")),
        out_specs=P(None, ("band", "ga"), None),
        check_vma=False,
    )
```

time: 390 us -> 339 us (0.87)
  Pallas kernels: 0 us -> 337 us
  waiting for transfers between devices: 302 us -> 0 us
  matrix products: 66.2 us -> 0 us
  between operations: 13.4 us -> 0.01 us
  local copies, waits for them, and re-layouts: 6.08 us -> 1.67 us
    pallas_call x0 -> x1, Pallas kernels: none -> 337 us  [per_device(): pl.pallas_call(functools.partial(kernel, chips, owners, strides), out_sha...]
    all_gather x2 -> x0, waiting for transfers between devices: 295 us -> none  [per_device(): piece = lax.all_gather(hx[:, :, first:last], 'band', axis=1, tiled=True)]
    dot_general x2 -> x0, matrix products: 66.2 us -> none  [contract(): lax.dot_general(left, right, (((1,), (1,)), ((), ())), precision=lax.Prec...]
    ppermute x1 -> x0, waiting for transfers between devices: 6.99 us -> none  [per_device(): result = result + lax.ppermute(block(lax.rem(me + step, n)), 'ga', ring)]
    slice x2 -> x0, local copies, waits for them, and re-layouts: 6.08 us -> none  [per_device(): piece = lax.all_gather(hx[:, :, first:last], 'band', axis=1, tiled=True)]
  transfers between devices with their start and end apart: 3 -> 0, of which waited for: 3 -> 0; matrix products, arithmetic and copies ran while one was open for 12% -> 0% of each run, Pallas kernels for 0% -> 0%
where the time goes in v1:
time: 339 us
  Pallas kernels  337 us (99%)
    pallas_call x1, Pallas kernels, per_device(): pl.pallas_call(functools.partial(kernel, chips, owners, strides), out_sha...  337 us

profile of v1, /device:TPU:0, one launch (start us, length us, event | category | flops | bytes accessed | tf_op | source)
XLA Modules:
  0.0 338.8 jit_solution(12424440241996057454)
XLA Ops:
  0.0 337.1 %shard_map.28 = (f32[2,128,256]{2,1,0:T(8,128)}, f32[7,2,16,32768]{3,2,1,0:T(8,128)}, f32[8,2,16,32768]{3,2,1,0:T(8,128)}) custom-call(f32[2,256,32768]{2,1,0:T(8,128)} %psi.1, f32[2,16,32768]{2,1,0:T(8,128)} %hx.1), custom_call_target="tpu_custom_call" | custom-call | tf_op jit(solution)/shard_map/pallas_call | solution.py:327
  337.1 1.7 copy.4

commit v2 on v1

--- a/solution.py
+++ b/solution.py
@@ -10,6 +10,8 @@
 CHUNKS = 8
 TILE = 512
 SLOTS = 3
+LAG = 19
+WIDE = 2048
 MESH = pl.DeviceIdType.MESH
 
 
@@ -311,12 +313,524 @@
         out[part] = jnp.concatenate(pieces[part], axis=1)
 
 
+def square_kernel(
+    strides,
+    psi,
+    hx,
+    out,
+    land,
+    twin,
+    lent,
+    psi_v,
+    hx_v,
+    acc,
+    final,
+    others,
+    lent_v,
+    lent_acc,
+    lent_out,
+    lent_in,
+    got,
+    twin_got,
+    side_sent,
+    end_sent,
+    twin_sent,
+    load_sem,
+    lent_load,
+    lent_sent,
+    lent_got,
+    back_sent,
+    back_got,
+    y_sent,
+    y_got,
+):
+    width = hx.shape[-1] // 16
+    vectors = hx.shape[1]
+    rows = psi.shape[1]
+    height = rows // 2
+    piece = height // 2
+    tile = min(WIDE, width)
+    x_stride, z_stride = strides
+
+    me = lax.axis_index("band")
+    y = lax.axis_index("ga")
+    core = lax.rem(me, 2)
+    chip = me // 2
+    x = lax.rem(chip // x_stride, 2)
+    z = lax.rem(chip // z_stride, 4)
+    far = z // 2
+    node = 3 * far + x * (1 - 2 * far)
+    end = lax.rem((z + 1) // 2 + 1, 2)
+    odd = lax.rem(node, 2)
+    sign = 1 - 2 * odd
+    mate = lax.rem(node + sign + 4, 4)
+    across = lax.rem(node - sign + 4, 4)
+    partner = me + 1 - 2 * core
+
+    def device_at(at, kind):
+        at_far = at // 2
+        at_x = lax.rem((at + 1) // 2, 2)
+        at_z = (1 - kind) * (1 + at_far) + kind * 3 * at_far
+        return 2 * (at_x * x_stride + at_z * z_stride) + core
+
+    inner_mate, inner_across = device_at(mate, 0), device_at(across, 0)
+    end_mate, own_end, own_inner = device_at(mate, 1), device_at(node, 1), device_at(node, 0)
+    inner, outer = end == 0, end == 1
+    mine = 2 * node + end
+
+    def columns(g):
+        return pl.ds(pl.multiple_of(g * width, 128), width)
+
+    def piece_of(q, way):
+        return 2 * q + lax.rem(way + odd, 2)
+
+    def node_at(way, d):
+        return lax.rem(node + (2 * way - 1) * sign * d + 12, 4)
+
+    def remote(source, to, dst, send, recv):
+        return pltpu.make_async_remote_copy(
+            src_ref=source,
+            dst_ref=dst,
+            send_sem=send,
+            recv_sem=recv,
+            device_id={"band": to, "ga": y},
+            device_id_type=MESH,
+        )
+
+    def block_copy(source, src, g, to, send):
+        return remote(
+            source, to, land.at[src, :, :, columns(g)], send.at[src, g], got.at[src, g]
+        )
+
+    def twin_copy(source, src, g):
+        return remote(
+            source,
+            partner,
+            twin.at[src, :, :, columns(g)],
+            twin_sent.at[src, g],
+            twin_got.at[src, g],
+        )
+
+    def distance(way, kind, block):
+        return lax.rem(block + 5 - kind - (end if way == 0 else 0), 4)
+
+    def unit(t, pos):
+        way = 0 if isinstance(pos, int) and pos == 0 else 1
+        index = t
+        if way:
+            index = (1 - end) * t + end * (2 * (t - LAG) + pos - 1)
+        block, q = index // 8, lax.rem(index, 8)
+        valid = (index >= 0) & (index < 32) & (inner | (q >= 1))
+        if way:
+            valid &= outer | (pos == 1)
+        return way, q, (distance(way, 0, block), distance(way, 1, block)), valid
+
+    def own_of(kind, d):
+        return (end == kind) & (d == 0)
+
+    def start_or_end(copy, begin):
+        copy.start() if begin else copy.wait_send()
+
+    def pass_one(way, index, kind, valid, begin):
+        block, q = index // 8, lax.rem(index, 8)
+        d = distance(way, kind, block)
+        g = piece_of(q, way)
+        src = 2 * node_at(way, d) + kind
+
+        @pl.when(valid & (inner | (q >= 1)) & jnp.logical_not(own_of(kind, d)))
+        def _():
+            held = land.at[src, :, :, columns(g)]
+            if begin:
+                block_copy(held, src, g, own_inner, side_sent).wait_recv()
+
+            def send(to, semaphore):
+                start_or_end(block_copy(held, src, g, to, semaphore), begin)
+
+            down = (q >= 1) if way == 0 else (q == 1)
+            sideways = outer & (q >= 2)
+            if kind == 1:
+                down &= (d >= 1 + way) & (d <= 2 + way)
+                sideways &= d < 3
+            onward = inner_mate if way == 0 else inner_across
+            pl.when(inner & (d < 3))(lambda: send(onward, side_sent))
+            pl.when(inner & down)(lambda: send(own_end, end_sent))
+            if way == 0:
+                pl.when(sideways)(lambda: send(end_mate, side_sent))
+            start_or_end(twin_copy(held, src, g), begin)
+
+    def pass_on(t, begin):
+        in_step, end_step, end_late = (t + 28) // 32, (t + 16) // 32, (t + 12) // 32
+        for_inner = 2 * t + in_step * (4 - t)
+        for_end = t + end_step * (t - 16) + end_late * (20 - t)
+        first = (1 - end) * for_inner + end * for_end
+        second = 2 * t + 1 - 16 * end
+        two = (inner & (t < 4)) | (outer & (t >= 16) & (t < 20))
+        for way in range(2):
+            fits = inner if way else True
+            pass_one(way, first, 0, (t < 20 + 8 * end) & fits, begin)
+            pass_one(way, second, 0, two & fits, begin)
+        for way in range(2):
+            fits = inner if way else True
+            pass_one(way, t, 1, (t < 32) & fits, begin)
+        for pos in range(2):
+            index = 2 * (t - LAG) + pos
+            for kind in range(2):
+                pass_one(1, index, kind, outer & (index >= 0) & (index < 32), begin)
+
+    def owner_of(k):
+        own = k // 2
+        return (1 - own) * (1 - y) + own * y
+
+    def lend(k):
+        begin = pl.multiple_of(owner_of(k) * height + lax.rem(k, 2) * piece, 8)
+        return remote(
+            psi.at[:, pl.ds(begin, piece), pl.ds(0, 2 * width)],
+            own_inner,
+            lent.at[k],
+            lent_sent.at[k],
+            lent_got.at[k],
+        )
+
+    def opening(begin):
+        def one(q, carry):
+            for way in range(2):
+                g = piece_of(q, way)
+                source = hx.at[:, :, columns(g)]
+
+                @pl.when(inner)
+                def _():
+                    to = inner_mate if way == 0 else inner_across
+                    start_or_end(block_copy(source, mine, g, to, side_sent), begin)
+                    pl.when((q >= 1) if way == 0 else (q == 1))(
+                        lambda: start_or_end(
+                            block_copy(source, mine, g, own_end, end_sent), begin
+                        )
+                    )
+
+                @pl.when(outer)
+                def _():
+                    start_or_end(block_copy(source, mine, g, own_inner, end_sent), begin)
+                    pl.when(q >= 1)(
+                        lambda: start_or_end(
+                            block_copy(source, mine, g, end_mate, side_sent), begin
+                        )
+                    )
+
+                pl.when(inner | (q >= 1))(
+                    lambda: start_or_end(twin_copy(source, mine, g), begin)
+                )
+            return carry
+
+        lax.fori_loop(0, 8, one, 0)
+
+        @pl.when(outer)
+        def _():
+            for k in range(4):
+                start_or_end(lend(jnp.int32(k)), begin)
+
+    def hx_loads(dst, sems, src, g, kind, own, act):
+        cols = columns(g)
+        target = dst.at[kind, :, core]
+        if act == "wait":
+            pltpu.make_async_copy(hx.at[:, :, cols], target, sems.at[2 * kind]).wait()
+        else:
+            pl.when(own)(
+                lambda: pltpu.make_async_copy(
+                    hx.at[:, :, cols], target, sems.at[2 * kind]
+                ).start()
+            )
+            pl.when(jnp.logical_not(own))(
+                lambda: pltpu.make_async_copy(
+                    land.at[src, :, :, cols], target, sems.at[2 * kind]
+                ).start()
+            )
+        other = pltpu.make_async_copy(
+            twin.at[src, :, :, cols], dst.at[kind, :, 1 - core], sems.at[2 * kind + 1]
+        )
+        other.wait() if act == "wait" else other.start()
+
+    def loads(t, act):
+        slot = lax.rem(t, 2)
+        for pos in range(3):
+            way, q, distances, valid = unit(t, pos)
+            g = piece_of(q, way)
+
+            @pl.when(valid)
+            def _(pos=pos, way=way, distances=distances, g=g):
+                sems = load_sem.at[slot, pos]
+                weights = pltpu.make_async_copy(
+                    psi.at[:, :, columns(g)], psi_v.at[slot, pos], sems.at[4]
+                )
+                weights.start()
+                for kind in range(2):
+                    src = 2 * node_at(way, distances[kind]) + kind
+                    source = hx.at[:, :, columns(g)]
+                    twin_copy(source, src, g).wait_recv()
+                    own = own_of(kind, distances[kind])
+                    hx_loads(hx_v.at[slot, pos], sems, src, g, kind, own, act)
+
+    def multiply(left_ref, right_ref, total_ref, first_at, second_at):
+        def body(k, carry):
+            cols = pl.ds(pl.multiple_of(k * tile, 128), tile)
+            first, second = [], []
+            for kind in range(2):
+                real = right_ref[kind, 0, :, :, cols].reshape(2 * vectors, tile)
+                imag = right_ref[kind, 1, :, :, cols].reshape(2 * vectors, tile)
+                real_high, real_low = split(real)
+                imag_high, imag_low = split(imag)
+                first += [real_high, imag_high, real_low, imag_low]
+                second += [imag_high, -real_high, imag_low, -real_low]
+            total = None
+            for part, right in ((0, first), (1, second)):
+                left = jnp.concatenate(split(left_ref[part, :, cols]), axis=0)
+                term = lax.dot_general(
+                    left,
+                    jnp.concatenate(right, axis=0),
+                    (((1,), (1,)), ((), ())),
+                    preferred_element_type=jnp.float32,
+                )
+                total = term if total is None else total + term
+            high = total.shape[0] // 2
+            total = total[:high] + total[high:]
+            lanes = 8 * vectors
+            total_ref[first_at] += total[:, :lanes]
+            total_ref[second_at] += total[:, lanes:]
+            return carry
+
+        if width == tile:
+            body(0, 0)
+        else:
+            lax.fori_loop(0, width // tile, body, 0)
+
+    def compute(t, pos):
+        slot = lax.rem(t, 2)
+        way, q, distances, valid = unit(t, pos)
+        g = piece_of(q, way)
+
+        @pl.when(valid)
+        def _():
+            sems = load_sem.at[slot, pos]
+            pltpu.make_async_copy(
+                psi.at[:, :, columns(g)], psi_v.at[slot, pos], sems.at[4]
+            ).wait()
+            at = []
+            for kind in range(2):
+                src = 2 * node_at(way, distances[kind]) + kind
+                hx_loads(hx_v.at[slot, pos], sems, src, g, kind, None, "wait")
+                at.append(src)
+            multiply(psi_v.at[slot, pos], hx_v.at[slot, pos], acc, at[0], at[1])
+
+    def fold(value):
+        half = 4 * vectors
+        return value[:, :half] + value[:, half:]
+
+    def back(k):
+        return pltpu.make_async_remote_copy(
+            src_ref=lent_out.at[k],
+            dst_ref=lent_in.at[k],
+            send_sem=back_sent.at[k],
+            recv_sem=back_got.at[k],
+            device_id={"band": own_end, "ga": owner_of(k)},
+            device_id_type=MESH,
+        )
+
+    def serve(k, begin, stop):
+        pl.when(begin == 0)(lambda: lend(k).wait_recv())
+
+        def places(v):
+            way, block = lax.rem(v, 2), v // 2
+            return [
+                (2 * node_at(way, d) + kind, own_of(kind, d))
+                for kind, d in ((0, lax.rem(block + 1, 4)), (1, block))
+            ]
+
+        def fetch(v, act):
+            g, slot = piece_of(0, lax.rem(v, 2)), lax.rem(v, 2)
+            sems = lent_load.at[slot]
+            weights = pltpu.make_async_copy(
+                lent.at[k, :, :, columns(g)], lent_v.at[slot], sems.at[4]
+            )
+            weights.wait() if act == "wait" else weights.start()
+            for kind, (src, own) in enumerate(places(v)):
+                hx_loads(hx_v.at[slot, 2], sems, src, g, kind, own, act)
+
+        fetch(begin, "start")
+
+        def one(v, carry):
+            pl.when(v + 1 < stop)(lambda: fetch(v + 1, "start"))
+            fetch(v, "wait")
+            slot = lax.rem(v, 2)
+            (first, _), (second, _) = places(v)
+            multiply(
+                lent_v.at[slot], hx_v.at[slot, 2], lent_acc.at[k], first, second
+            )
+            return carry
+
+        lax.fori_loop(begin, stop, one, 0)
+
+        @pl.when(stop == 8)
+        def _():
+            for at in range(4):
+                lent_out[k, at] = jnp.concatenate(
+                    [fold(lent_acc[k, 2 * at]), fold(lent_acc[k, 2 * at + 1])], axis=1
+                )
+            back(k).start()
+
+    barrier = pltpu.get_barrier_semaphore()
+
+    def greet(to, at_y):
+        pl.semaphore_signal(
+            barrier, inc=1, device_id={"band": to, "ga": at_y}, device_id_type=MESH
+        )
+
+    greet(partner, y)
+    greet(me, 1 - y)
+
+    @pl.when(inner)
+    def _():
+        for to in (inner_mate, inner_across, own_end):
+            greet(to, y)
+        greet(own_end, 1 - y)
+        pl.semaphore_wait(barrier, 6)
+
+    @pl.when(outer)
+    def _():
+        for to in (end_mate, own_inner):
+            greet(to, y)
+        greet(own_inner, 1 - y)
+        pl.semaphore_wait(barrier, 5)
+
+    opening(True)
+    acc[...] = jnp.zeros_like(acc)
+    lent_acc[...] = jnp.zeros_like(lent_acc)
+
+    def tick(t, carry):
+        pl.when(t >= 2)(lambda: compute(t - 2, 0))
+        pl.when(t >= 1)(lambda: loads(t - 1, "start"))
+
+        def later(pos, carry):
+            compute(t - 2, pos)
+            return carry
+
+        @pl.when(t >= 2)
+        def _():
+            lax.fori_loop(1, 3, later, 0)
+
+        pass_on(t, True)
+
+        early = (t == 18) | (t == 21) | (t == 24)
+        late = (t >= 26) & (t < 29)
+        last = t == 34
+        k = jnp.where(early, (t - 18) // 3, jnp.where(late, t - 26, 3))
+        begin = jnp.where(late, 6, 0)
+        stop = jnp.where(early, 6, 8)
+        pl.when(inner & (early | late | last))(lambda: serve(k, begin, stop))
+        return carry
+
+    lax.fori_loop(0, 18 + LAG, tick, 0)
+
+    for at in range(4):
+        final[at] = jnp.concatenate([fold(acc[2 * at]), fold(acc[2 * at + 1])], axis=1)
+
+    theirs = pl.ds(pl.multiple_of((1 - y) * height, 8), height)
+    ours = pl.ds(pl.multiple_of(y * height, 8), height)
+
+    def y_copy(at):
+        return pltpu.make_async_remote_copy(
+            src_ref=final.at[at, theirs],
+            dst_ref=others.at[at],
+            send_sem=y_sent.at[at],
+            recv_sem=y_got.at[at],
+            device_id={"band": me, "ga": 1 - y},
+            device_id_type=MESH,
+        )
+
+    for at in range(4):
+        y_copy(at).start()
+
+    opening(False)
+
+    def closing(t, carry):
+        pass_on(t, False)
+        return carry
+
+    lax.fori_loop(0, 16 + LAG, closing, 0)
+    for at in range(4):
+        y_copy(at).wait_recv()
+        final[at, ours] += others[at]
+
+    @pl.when(outer)
+    def _():
+        for k in range(4):
+            back(jnp.int32(k)).wait_recv()
+            start = pl.multiple_of(y * height + (k % 2) * piece, 8)
+            for at in range(4):
+                final[at, pl.ds(start, piece)] += lent_in[k, at]
+
+    for part in range(2):
+        pieces = []
+        for j in range(8):
+            at_x, at_z = (j // x_stride) % 2, (j // z_stride) % 4
+            at_far, kind = at_z // 2, ((at_z + 1) // 2 + 1) % 2
+            at = 3 * at_far + at_x * (1 - 2 * at_far)
+            begin = (2 * kind + part) * 2 * vectors
+            pieces.append(final[at, ours][:, begin : begin + 2 * vectors])
+        out[part] = jnp.concatenate(pieces, axis=1)
+    for at in range(4):
+        y_copy(at).wait_send()
+
+    @pl.when(inner)
+    def _():
+        for k in range(4):
+            back(jnp.int32(k)).wait_send()
+
+
 def solution(mesh):
     chips = mesh.shape["band"] // 2
     owners = mesh.shape["ga"]
     strides = ladder(mesh)
 
-    def per_device(psi, hx):
+    def by_square(psi, hx):
+        parts, rows, depth = psi.shape
+        vectors = hx.shape[1]
+        height = rows // 2
+        width = depth // 16
+        lanes = 8 * vectors
+        dma = pltpu.SemaphoreType.DMA
+        whole = pl.BlockSpec(memory_space=pl.ANY)
+        lent = (4, parts, height // 2, 2 * width)
+        result, *_ = pl.pallas_call(
+            functools.partial(square_kernel, strides),
+            out_shape=(
+                jax.ShapeDtypeStruct((parts, height, 16 * vectors), jnp.float32),
+                jax.ShapeDtypeStruct((8, *hx.shape), jnp.float32),
+                jax.ShapeDtypeStruct((8, *hx.shape), jnp.float32),
+                jax.ShapeDtypeStruct(lent, jnp.float32),
+            ),
+            in_specs=[whole] * 2,
+            out_specs=(pl.BlockSpec(memory_space=pltpu.VMEM), whole, whole, whole),
+            scratch_shapes=[
+                pltpu.VMEM((2, 3, parts, rows, width), jnp.float32),
+                pltpu.VMEM((2, 3, 2, parts, 2, vectors, width), jnp.float32),
+                pltpu.VMEM((8, rows, lanes), jnp.float32),
+                pltpu.VMEM((4, rows, lanes), jnp.float32),
+                pltpu.VMEM((4, height, lanes), jnp.float32),
+                pltpu.VMEM((2, parts, height // 2, width), jnp.float32),
+                pltpu.VMEM((4, 8, height // 2, lanes), jnp.float32),
+                pltpu.VMEM((4, 4, height // 2, lanes), jnp.float32),
+                pltpu.VMEM((4, 4, height // 2, lanes), jnp.float32),
+                *[dma((8, 16))] * 5,
+                dma((2, 3, 5)),
+                dma((2, 5)),
+                *[dma((4,))] * 6,
+            ],
+            compiler_params=pltpu.CompilerParams(
+                collective_id=0, has_side_effects=True, vmem_limit_bytes=60 * 2**20
+            ),
+        )(psi, hx)
+        return result
+
+    def by_ring(psi, hx):
         parts, rows, depth = psi.shape
         vectors = hx.shape[1]
         height = rows // owners
@@ -360,7 +874,7 @@
         return result
 
     return jax.shard_map(
-        per_device,
+        by_square if (chips, owners) == (8, 2) else by_ring,
         mesh=mesh,
         in_specs=(P(None, "band", "ga"), P(None, "band", "ga")),
         out_specs=P(None, ("band", "ga"), None),

time: 339 us -> 323 us (0.953)
  Pallas kernels: 337 us -> 318 us
    pallas_call x1, Pallas kernels: 337 us -> 318 us  [by_square(): pl.pallas_call(functools.partial(square_kernel, strides), out_shape=(jax....]
where the time goes in v2:
time: 323 us; the launch traced here: 320 us
  Pallas kernels  318 us (98%)
    pallas_call x1, Pallas kernels, by_square(): pl.pallas_call(functools.partial(square_kernel, strides), out_shape=(jax....  318 us

profile of v2, /device:TPU:0, one launch (start us, length us, event | category | flops | bytes accessed | tf_op | source)
XLA Modules:
  0.0 320.1 jit_solution(13236794689835381211)
XLA Ops:
  0.0 318.5 %shard_map.28 = (f32[2,128,256]{2,1,0:T(8,128)}, f32[8,2,16,32768]{3,2,1,0:T(8,128)}, f32[8,2,16,32768]{3,2,1,0:T(8,128)}, f32[4,2,64,4096]{3,2,1,0:T(8,128)}) custom-call(f32[2,256,32768]{2,1,0:T(8,128)} %psi.1, f32[2,16,32768]{2,1,0:T(8,128)} %hx.1), custom_call_target="tpu_custom_call" | custom-call | tf_op jit(solution)/shard_map/pallas_call | solution.py:802
  318.5 1.7 copy.4

commit v3 on v2

--- a/solution.py
+++ b/solution.py
@@ -327,6 +327,7 @@
     final,
     others,
     lent_v,
+    lent_hx,
     lent_acc,
     lent_out,
     lent_in,
@@ -399,7 +400,7 @@
 
     def block_copy(source, src, g, to, send):
         return remote(
-            source, to, land.at[src, :, :, columns(g)], send.at[src, g], got.at[src, g]
+            source, to, land.at[src, :, :, columns(g)], send, got.at[src, g]
         )
 
     def twin_copy(source, src, g):
@@ -407,7 +408,7 @@
             source,
             partner,
             twin.at[src, :, :, columns(g)],
-            twin_sent.at[src, g],
+            twin_sent,
             twin_got.at[src, g],
         )
 
@@ -428,10 +429,7 @@
     def own_of(kind, d):
         return (end == kind) & (d == 0)
 
-    def start_or_end(copy, begin):
-        copy.start() if begin else copy.wait_send()
-
-    def pass_one(way, index, kind, valid, begin):
+    def pass_one(way, index, kind, valid):
         block, q = index // 8, lax.rem(index, 8)
         d = distance(way, kind, block)
         g = piece_of(q, way)
@@ -440,11 +438,10 @@
         @pl.when(valid & (inner | (q >= 1)) & jnp.logical_not(own_of(kind, d)))
         def _():
             held = land.at[src, :, :, columns(g)]
-            if begin:
-                block_copy(held, src, g, own_inner, side_sent).wait_recv()
+            block_copy(held, src, g, own_inner, side_sent).wait_recv()
 
             def send(to, semaphore):
-                start_or_end(block_copy(held, src, g, to, semaphore), begin)
+                block_copy(held, src, g, to, semaphore).start()
 
             down = (q >= 1) if way == 0 else (q == 1)
             sideways = outer & (q >= 2)
@@ -456,9 +453,9 @@
             pl.when(inner & down)(lambda: send(own_end, end_sent))
             if way == 0:
                 pl.when(sideways)(lambda: send(end_mate, side_sent))
-            start_or_end(twin_copy(held, src, g), begin)
-
-    def pass_on(t, begin):
+            twin_copy(held, src, g).start()
+
+    def pass_on(t):
         in_step, end_step, end_late = (t + 28) // 32, (t + 16) // 32, (t + 12) // 32
         for_inner = 2 * t + in_step * (4 - t)
         for_end = t + end_step * (t - 16) + end_late * (20 - t)
@@ -467,15 +464,15 @@
         two = (inner & (t < 4)) | (outer & (t >= 16) & (t < 20))
         for way in range(2):
             fits = inner if way else True
-            pass_one(way, first, 0, (t < 20 + 8 * end) & fits, begin)
-            pass_one(way, second, 0, two & fits, begin)
+            pass_one(way, first, 0, (t < 20 + 8 * end) & fits)
+            pass_one(way, second, 0, two & fits)
         for way in range(2):
             fits = inner if way else True
-            pass_one(way, t, 1, (t < 32) & fits, begin)
+            pass_one(way, t, 1, (t < 32) & fits)
         for pos in range(2):
             index = 2 * (t - LAG) + pos
             for kind in range(2):
-                pass_one(1, index, kind, outer & (index >= 0) & (index < 32), begin)
+                pass_one(1, index, kind, outer & (index >= 0) & (index < 32))
 
     def owner_of(k):
         own = k // 2
@@ -491,33 +488,23 @@
             lent_got.at[k],
         )
 
-    def opening(begin):
+    def opening():
         def one(q, carry):
             for way in range(2):
                 g = piece_of(q, way)
                 source = hx.at[:, :, columns(g)]
 
-                @pl.when(inner)
-                def _():
-                    to = inner_mate if way == 0 else inner_across
-                    start_or_end(block_copy(source, mine, g, to, side_sent), begin)
-                    pl.when((q >= 1) if way == 0 else (q == 1))(
-                        lambda: start_or_end(
-                            block_copy(source, mine, g, own_end, end_sent), begin
-                        )
-                    )
-
-                @pl.when(outer)
-                def _():
-                    start_or_end(block_copy(source, mine, g, own_inner, end_sent), begin)
-                    pl.when(q >= 1)(
-                        lambda: start_or_end(
-                            block_copy(source, mine, g, end_mate, side_sent), begin
-                        )
-                    )
-
+                def send(to, semaphore):
+                    block_copy(source, mine, g, to, semaphore).start()
+
+                onward = inner_mate if way == 0 else inner_across
+                down = (q >= 1) if way == 0 else (q == 1)
+                pl.when(inner)(lambda: send(onward, side_sent))
+                pl.when(inner & down)(lambda: send(own_end, end_sent))
+                pl.when(outer)(lambda: send(own_inner, end_sent))
+                pl.when(outer & (q >= 1))(lambda: send(end_mate, side_sent))
                 pl.when(inner | (q >= 1))(
-                    lambda: start_or_end(twin_copy(source, mine, g), begin)
+                    lambda: twin_copy(source, mine, g).start()
                 )
             return carry
 
@@ -526,7 +513,7 @@
         @pl.when(outer)
         def _():
             for k in range(4):
-                start_or_end(lend(jnp.int32(k)), begin)
+                lend(jnp.int32(k)).start()
 
     def hx_loads(dst, sems, src, g, kind, own, act):
         cols = columns(g)
@@ -634,8 +621,11 @@
             device_id_type=MESH,
         )
 
-    def serve(k, begin, stop):
-        pl.when(begin == 0)(lambda: lend(k).wait_recv())
+    def serve(first_k, late, stop):
+        pl.when(late == 0)(lambda: lend(first_k).wait_recv())
+
+        def job(u):
+            return first_k + late * (u // 2), u + late * (6 - 2 * (u // 2))
 
         def places(v):
             way, block = lax.rem(v, 2), v // 2
@@ -644,37 +634,44 @@
                 for kind, d in ((0, lax.rem(block + 1, 4)), (1, block))
             ]
 
-        def fetch(v, act):
-            g, slot = piece_of(0, lax.rem(v, 2)), lax.rem(v, 2)
+        def fetch(u, act):
+            k, v = job(u)
+            g, slot = piece_of(0, lax.rem(v, 2)), lax.rem(u, 3)
             sems = lent_load.at[slot]
             weights = pltpu.make_async_copy(
                 lent.at[k, :, :, columns(g)], lent_v.at[slot], sems.at[4]
             )
             weights.wait() if act == "wait" else weights.start()
             for kind, (src, own) in enumerate(places(v)):
-                hx_loads(hx_v.at[slot, 2], sems, src, g, kind, own, act)
-
-        fetch(begin, "start")
-
-        def one(v, carry):
-            pl.when(v + 1 < stop)(lambda: fetch(v + 1, "start"))
-            fetch(v, "wait")
-            slot = lax.rem(v, 2)
+                hx_loads(lent_hx.at[slot], sems, src, g, kind, own, act)
+
+        fetch(jnp.int32(0), "start")
+        fetch(jnp.int32(1), "start")
+
+        def one(u, carry):
+            pl.when(u + 2 < stop)(lambda: fetch(u + 2, "start"))
+            fetch(u, "wait")
+            k, v = job(u)
+            slot = lax.rem(u, 3)
             (first, _), (second, _) = places(v)
-            multiply(
-                lent_v.at[slot], hx_v.at[slot, 2], lent_acc.at[k], first, second
-            )
+            multiply(lent_v.at[slot], lent_hx.at[slot], lent_acc.at[k], first, second)
             return carry
 
-        lax.fori_loop(begin, stop, one, 0)
-
-        @pl.when(stop == 8)
-        def _():
+        lax.fori_loop(0, stop, one, 0)
+
+        def give(k):
             for at in range(4):
                 lent_out[k, at] = jnp.concatenate(
                     [fold(lent_acc[k, 2 * at]), fold(lent_acc[k, 2 * at + 1])], axis=1
                 )
-            back(k).start()
+            back(jnp.int32(k)).start()
+
+        @pl.when(late == 1)
+        def _():
+            for k in range(3):
+                give(k)
+
+        pl.when(stop == 8)(lambda: give(3))
 
     barrier = pltpu.get_barrier_semaphore()
 
@@ -700,7 +697,7 @@
         greet(own_inner, 1 - y)
         pl.semaphore_wait(barrier, 5)
 
-    opening(True)
+    opening()
     acc[...] = jnp.zeros_like(acc)
     lent_acc[...] = jnp.zeros_like(lent_acc)
 
@@ -716,15 +713,14 @@
         def _():
             lax.fori_loop(1, 3, later, 0)
 
-        pass_on(t, True)
-
-        early = (t == 18) | (t == 21) | (t == 24)
-        late = (t >= 26) & (t < 29)
+        pass_on(t)
+
+        early = (t == 17) | (t == 18) | (t == 23)
+        late = jnp.where(t == 26, 1, 0)
         last = t == 34
-        k = jnp.where(early, (t - 18) // 3, jnp.where(late, t - 26, 3))
-        begin = jnp.where(late, 6, 0)
-        stop = jnp.where(early, 6, 8)
-        pl.when(inner & (early | late | last))(lambda: serve(k, begin, stop))
+        k = jnp.where(early, (t - 16) // 3 + t // 18 - t // 23, 3 - 3 * late)
+        stop = jnp.where(last, 8, 6)
+        pl.when(inner & (early | (t == 26) | last))(lambda: serve(k, late, stop))
         return carry
 
     lax.fori_loop(0, 18 + LAG, tick, 0)
@@ -748,13 +744,24 @@
     for at in range(4):
         y_copy(at).start()
 
-    opening(False)
-
-    def closing(t, carry):
-        pass_on(t, False)
-        return carry
-
-    lax.fori_loop(0, 16 + LAG, closing, 0)
+    def sent(semaphore, *refs):
+        for ref in refs:
+            pltpu.make_async_copy(ref, ref, semaphore).wait()
+
+    @pl.when(inner)
+    def _():
+        sent(side_sent, land.at[pl.ds(0, 6)])
+        sent(end_sent, land.at[pl.ds(0, 3)])
+        sent(twin_sent, land)
+
+    @pl.when(outer)
+    def _():
+        sent(side_sent, land.at[pl.ds(0, 3)], land.at[0, :, :, pl.ds(0, 2 * width)])
+        sent(end_sent, land.at[0])
+        sent(twin_sent, land.at[pl.ds(0, 7)])
+        for k in range(4):
+            lend(jnp.int32(k)).wait_send()
+
     for at in range(4):
         y_copy(at).wait_recv()
         final[at, ours] += others[at]
@@ -815,13 +822,15 @@
                 pltpu.VMEM((8, rows, lanes), jnp.float32),
                 pltpu.VMEM((4, rows, lanes), jnp.float32),
                 pltpu.VMEM((4, height, lanes), jnp.float32),
-                pltpu.VMEM((2, parts, height // 2, width), jnp.float32),
+                pltpu.VMEM((3, parts, height // 2, width), jnp.float32),
+                pltpu.VMEM((3, 2, parts, 2, vectors, width), jnp.float32),
                 pltpu.VMEM((4, 8, height // 2, lanes), jnp.float32),
                 pltpu.VMEM((4, 4, height // 2, lanes), jnp.float32),
                 pltpu.VMEM((4, 4, height // 2, lanes), jnp.float32),
-                *[dma((8, 16))] * 5,
+                *[dma((8, 16))] * 2,
+                *[dma] * 3,
                 dma((2, 3, 5)),
-                dma((2, 5)),
+                dma((3, 5)),
                 *[dma((4,))] * 6,
             ],
             compiler_params=pltpu.CompilerParams(

time: 323 us -> 314 us (0.972)
  Pallas kernels: 318 us -> 312 us
    pallas_call x1, Pallas kernels: 318 us -> 312 us  [by_square(): pl.pallas_call(functools.partial(square_kernel, strides), out_shape=(jax....]
where the time goes in v3:
time: 314 us; the launch traced here: 313 us
  Pallas kernels  312 us (99%)
    pallas_call x1, Pallas kernels, by_square(): pl.pallas_call(functools.partial(square_kernel, strides), out_shape=(jax....  312 us

profile of v3, /device:TPU:0, one launch (start us, length us, event | category | flops | bytes accessed | tf_op | source)
XLA Modules:
  0.0 313.4 jit_solution(13003346507924942602)
XLA Ops:
  0.0 311.7 %shard_map.28 = (f32[2,128,256]{2,1,0:T(8,128)}, f32[8,2,16,32768]{3,2,1,0:T(8,128)}, f32[8,2,16,32768]{3,2,1,0:T(8,128)}, f32[4,2,64,4096]{3,2,1,0:T(8,128)}) custom-call(f32[2,256,32768]{2,1,0:T(8,128)} %psi.1, f32[2,16,32768]{2,1,0:T(8,128)} %hx.1), custom_call_target="tpu_custom_call" | custom-call | tf_op jit(solution)/shard_map/pallas_call | solution.py:809
  311.7 1.7 copy.4
